TPU v7x, 256 devices: a whole 4x4x8 slice. The times are simulated.
256 devices in a mesh: path: 128 (over y, z_hi, x, core), shard: 2 (over z_lo).
Axes of the slice: x: 4, y: 4, z: 8 (z_hi: 4, z_lo: 2; z = z_hi * 2 + z_lo), core: 2. Of those that a mesh axis runs over, the one named last changes fastest.
Arguments:
- features: bfloat16 [128, 512, 768], P('path', None, 'shard'), may hold values from -6 to 6
- path_weights: bfloat16 [128, 768, 3072], P('path', None, 'shard'), may hold values from -6 to 6
- cotangent: bfloat16 [128, 512, 3072], P('path', None, 'shard'), may hold values from -6 to 6
- path_module: int32 [128, 1], replicated, may hold values from 0 to 15
- outer_params: float32 [16, 768, 3072], P(None, 'path', 'shard'), may hold values from -6 to 6
- outer_moment: float32 [16, 768, 3072], P(None, 'path', 'shard'), may hold values from -2 to 2
Outputs:
- synced: bfloat16 [128, 768, 3072], P('path', None, 'shard')
- params_new: float32 [16, 768, 3072], P(None, 'path', 'shard')
- moment_new: float32 [16, 768, 3072], P(None, 'path', 'shard')
- grad_weight: bfloat16 [128, 768, 3072], P('path', None, 'shard')
- grad_input: bfloat16 [128, 512, 768], P('path', None, 'shard')
Inputs may be any that keep to these rules, and one draw needn't show every extreme that they name: `path_module`: every module id is used by at least one path.
All inputs are finite; a program needn't handle non-finite values.
Results may differ from a plain program's by a relative error of at most 0.005.
Values may be sent and summed in bfloat16 or wider, within the bound.
No kernel may reach another device: no remote copies, remote signals or barrier semaphores. Data moves between devices by JAX's collectives and lax.ppermute only.
A program may use at most 64 MiB of HBM per device.

v0:
```python
import jax
import jax.numpy as jnp
from jax import lax
from jax.sharding import PartitionSpec as P

D = 768
MODULES = 16


outer_momentum = 0.9
outer_rate = 0.7


def silu_slope(pre):
    sigmoid_part = jax.nn.sigmoid(pre)
    return sigmoid_part * (1.0 + pre * (1.0 - sigmoid_part))


def on_device(features, path_weights, cotangent, path_module, outer_params, outer_moment):
    multiplier = D ** (-0.5)
    weights_here = path_weights[0]
    count_path = lax.axis_size("path")
    received = lax.all_to_all(weights_here, "path", split_axis=0, concat_axis=0, tiled=True)
    flattened = received.reshape(count_path, -1)
    modules = path_module[:, 0]
    member = modules[None, :] == jnp.arange(MODULES, dtype=jnp.int32)[:, None]
    summed = jnp.dot(member.astype(jnp.bfloat16), flattened, preferred_element_type=jnp.float32)
    counts = jnp.sum(member.astype(jnp.float32), axis=1)
    average = summed / counts[:, None]
    shaped = outer_params.reshape(MODULES, -1)
    pseudo = shaped - average
    moment_flat = outer_momentum * outer_moment.reshape(MODULES, -1) + pseudo
    params_flat = shaped - outer_rate * (pseudo + outer_momentum * moment_flat)
    chosen = jnp.dot(
        member.T.astype(jnp.bfloat16),
        params_flat.astype(jnp.bfloat16),
        preferred_element_type=jnp.float32,
    )
    chosen = chosen.astype(jnp.bfloat16).reshape(received.shape)
    returned = lax.all_to_all(chosen, "path", split_axis=0, concat_axis=0, tiled=True)
    synced = returned[None]
    params_new = params_flat.reshape(outer_params.shape)
    moment_new = moment_flat.reshape(outer_moment.shape)
    tokens_full = lax.all_gather(features, "shard", axis=2, tiled=True)[0]
    pre = jnp.dot(tokens_full, weights_here, preferred_element_type=jnp.float32) * multiplier
    delta = (cotangent[0].astype(jnp.float32) * silu_slope(pre)).astype(jnp.bfloat16)
    grad_w = lax.dot_general(
        tokens_full, delta, (((0,), (0,)), ((), ())), preferred_element_type=jnp.float32
    )
    grad_w = (grad_w * multiplier).astype(jnp.bfloat16)
    terms = lax.dot_general(
        delta, weights_here, (((1,), (1,)), ((), ())), preferred_element_type=jnp.float32
    )
    terms = terms * multiplier
    grad_in = lax.psum_scatter(terms, "shard", scatter_dimension=1, tiled=True).astype(jnp.bfloat16)
    grad_weight = grad_w[None]
    grad_input = grad_in[None]
    return (synced, params_new, moment_new, grad_weight, grad_input)


def solution(mesh):
    return jax.shard_map(
        on_device,
        mesh=mesh,
        in_specs=(
            P("path", None, "shard"),
            P("path", None, "shard"),
            P("path", None, "shard"),
            P(),
            P(None, "path", "shard"),
            P(None, "path", "shard"),
        ),
        out_specs=(
            P("path", None, "shard"),
            P(None, "path", "shard"),
            P(None, "path", "shard"),
            P("path", None, "shard"),
            P("path", None, "shard"),
        ),
        check_vma=False,
    )
```

profile of v0, /device:TPU:32, one launch (start us, length us, event | category | flops | bytes accessed | tf_op | source)
XLA Modules:
  0.0 236.4 jit_solution(12447965443789901729)
XLA Ops:
  7.2 4.9 %all_to_all.12 = bf16[128,6,1536]{2,1,0:T(8,128)(2,1)} reshape(bf16[1,768,1536]{2,1,0:T(8,128)(2,1)} %param.7) | data formatting | bytes 4718592 | tf_op jit(solution)/shard_map/all_to_all | solution.py:23
  12.1 14.9 %all-to-all-start = ((bf16[128,6,1536]{2,1,0:T(8,128)(2,1)}), bf16[128,6,1536]{2,1,0:T(8,128)(2,1)S(1)}, u32[]{:S(2)}, u32[]{:S(2)}) async-start(bf16[128,6,1536]{2,1,0:T(8,128)(2,1)} %all_to_all.12), calls=%async_computation | async-start | bytes 6291456 | tf_op jit(solution)/shard_map/all_to_all | solution.py:23
  27.0 0.0 copy-start.2
  27.0 0.0 copy-start.4
  27.0 0.0 copy-start.3
  27.0 1.2 multiply_bitcast_fusion
  28.2 0.9 copy.43
  29.1 0.9 copy.42
  29.9 0.1 convert_reduce_fusion
  30.1 73.8 %all_gather.3 = bf16[1,512,768]{2,1,0:T(8,128)(2,1)} all-gather(bf16[1,512,384]{2,1,0:T(8,128)(2,1)S(1)} %copy-done.3), channel_id=1, replica_groups=mesh['path'=128,'shard'=2] {'shard'}, dimensions={2}, use_global_device_ids=true | all-gather | bytes 1179648 | tf_op jit(solution)/shard_map/all_gather | solution.py:44
  103.9 0.6 all-to-all-done
  104.5 3.0 %copy.33 = bf16[128,6,1536]{0,2,1:T(8,128)(2,1)} copy(bf16[128,6,1536]{2,1,0:T(8,128)(2,1)S(1)} %all-to-all-done) | data formatting | bytes 4718592 | tf_op jit(solution)/shard_map/all_to_all | solution.py:23
  107.5 3.5 %multiply_subtract_fusion = (f32[16,9216]{1,0:T(8,128)S(1)}, f32[16,9216]{1,0:T(8,128)}) fusion(f32[16,9216]{1,0:T(8,128)} %bitcast.44, f32[16,9216]{1,0:T(8,128)} %bitcast.43, f32[16]{0:T(128)S(1)} %convert_reduce_fusion, bf16[128,9216]{0,1:T(8,128)(2,1)} %bitcast.40, s32[128]{0:T(128)S(1)} %bitcast.48), kind=kOutput, calls=%fused_computation.16 | convolution fusion | flops 38782976 | bytes 4719168 | tf_op jit(solution)/shard_map/dot_general | solution.py:27
  111.0 0.8 copy-done
  111.8 0.8 convolution_convert_fusion
  112.6 2.4 %copy.35 = bf16[128,9216]{0,1:T(8,128)(2,1)} copy(bf16[128,9216]{1,0:T(8,128)(2,1)S(1)} %convolution_convert_fusion) | data formatting | bytes 4718592 | tf_op jit(solution)/shard_map/convert_element_type | solution.py:39
  115.0 4.9 %copy.36 = bf16[128,6,1536]{2,1,0:T(8,128)(2,1)} copy(bf16[128,6,1536]{0,2,1:T(8,128)(2,1)} %bitcast.41) | data formatting | bytes 4718592 | tf_op jit(solution)/shard_map/all_to_all | solution.py:40
  120.0 13.1 %all-to-all-start.1 = ((bf16[128,6,1536]{2,1,0:T(8,128)(2,1)}), bf16[128,6,1536]{2,1,0:T(8,128)(2,1)S(1)}, u32[]{:S(2)}, u32[]{:S(2)}) async-start(bf16[128,6,1536]{2,1,0:T(8,128)(2,1)} %copy.36), calls=%async_computation.1 | async-start | bytes 6291456 | tf_op jit(solution)/shard_map/all_to_all | solution.py:40
  133.1 0.0 reduce-scatter.2.cloned.1.call-start
  133.1 0.0 copy-start.1
  133.2 4.7 %fusion.1 = bf16[512,1536]{1,0:T(8,128)(2,1)S(1)} fusion(bf16[1,768,1536]{2,1,0:T(8,128)(2,1)} %param.7, bf16[1,512,1536]{2,1,0:T(8,128)(2,1)} %param.8, bf16[1,512,768]{2,1,0:T(8,128)(2,1)} %all_gather.3), kind=kOutput, calls=%fused_computation.6 | convolution fusion | flops 1216610304 | bytes 6291456 | tf_op jit(solution)/shard_map/dot_general | solution.py:45
  137.9 0.0 copy-start.5
  137.9 1.1 copy-done.5
  139.0 2.6 %fusion.8 = f32[512,768]{1,0:T(8,128)} fusion(bf16[512,1536]{1,0:T(8,128)(2,1)S(1)} %fusion.1, bf16[1,768,1536]{2,1,0:T(8,128)(2,1)S(1)} %copy-done.1), kind=kOutput, calls=%fused_computation.11 | convolution fusion | flops 1208352768 | bytes 5505024 | tf_op jit(solution)/shard_map/dot_general | solution.py:51
  141.6 0.0 reduce-scatter.2.cloned.1.call-update
  141.6 4.4 %fusion.2 = bf16[1,768,1536]{1,2,0:T(8,128)(2,1)} fusion(bf16[512,1536]{1,0:T(8,128)(2,1)} %copy-done.5, bf16[1,512,768]{2,1,0:T(8,128)(2,1)} %all_gather.3), kind=kOutput, calls=%fused_computation.7 | convolution fusion | flops 1210318848 | bytes 4718592 | tf_op jit(solution)/shard_map/dot_general | solution.py:47
  146.0 4.3 %copy.39 = bf16[1,768,1536]{2,1,0:T(8,128)(2,1)} copy(bf16[1,768,1536]{1,2,0:T(8,128)(2,1)} %fusion.2) | data formatting | bytes 4718592
  150.3 61.6 %reduce-scatter.2.cloned.1.call-done = f32[512,384]{1,0:T(8,128)} async-done(((f32[512,768]{1,0:T(8,128)}), f32[512,384]{1,0:T(8,128)}) %reduce-scatter.2.cloned.1.call-update) | async-done | bytes 786448 | tf_op jit(solution)/shard_map/reduce_scatter | solution.py:55
  212.0 1.9 convert_bitcast_fusion
  213.9 2.3 copy_bitcast_fusion
  216.2 11.1 %all-to-all-done.1 = bf16[128,6,1536]{2,1,0:T(8,128)(2,1)S(1)} async-done(((bf16[128,6,1536]{2,1,0:T(8,128)(2,1)}), bf16[128,6,1536]{2,1,0:T(8,128)(2,1)S(1)}, u32[]{:S(2)}, u32[]{:S(2)}) %all-to-all-start.1) | async-done | bytes 2359328 | tf_op jit(solution)/shard_map/all_to_all | solution.py:40
  227.3 2.2 broadcast_in_dim.11
  (5 shorter events, 0.0 us)
Async XLA Ops:
  12.1 92.4 %all-to-all-start = ((bf16[128,6,1536]{2,1,0:T(8,128)(2,1)}), bf16[128,6,1536]{2,1,0:T(8,128)(2,1)S(1)}, u32[]{:S(2)}, u32[]{:S(2)}) async-start(bf16[128,6,1536]{2,1,0:T(8,128)(2,1)} %all_to_all.12), calls=%async_computation | async-start | bytes 6291456 | tf_op jit(solution)/shard_map/all_to_all | solution.py:23
  27.0 2.1 copy-start.2
  27.0 2.9 %copy-start.4 = (s32[128,1]{0,1:T(1,128)S(1)}, s32[128,1]{0,1:T(1,128)}, u32[]{:S(2)}) copy-start(s32[128,1]{0,1:T(1,128)} %param.9) | copy-start | bytes 1540
  27.0 3.1 %copy-start.3 = (bf16[1,512,384]{2,1,0:T(8,128)(2,1)S(1)}, bf16[1,512,384]{2,1,0:T(8,128)(2,1)}, u32[]{:S(2)}) copy-start(bf16[1,512,384]{2,1,0:T(8,128)(2,1)} %param.6) | copy-start | bytes 1179652
  111.0 0.8 copy-start
  120.0 107.4 %all-to-all-start.1 = ((bf16[128,6,1536]{2,1,0:T(8,128)(2,1)}), bf16[128,6,1536]{2,1,0:T(8,128)(2,1)S(1)}, u32[]{:S(2)}, u32[]{:S(2)}) async-start(bf16[128,6,1536]{2,1,0:T(8,128)(2,1)} %copy.36), calls=%async_computation.1 | async-start | bytes 6291456 | tf_op jit(solution)/shard_map/all_to_all | solution.py:40
  133.1 78.9 %reduce-scatter.2.cloned.1.call-start = ((), (), s32[]{:S(2)}) async-start(), calls=%async_computation.3 | async-start | bytes 2359296 | tf_op jit(solution)/shard_map/reduce_scatter | solution.py:55
  133.1 5.9 %copy-start.1 = (bf16[1,768,1536]{2,1,0:T(8,128)(2,1)S(1)}, bf16[1,768,1536]{2,1,0:T(8,128)(2,1)}, u32[]{:S(2)}) copy-start(bf16[1,768,1536]{2,1,0:T(8,128)(2,1)} %param.7) | copy-start | bytes 7077892
  137.9 1.1 copy-start.5
Sparse Core Ops, SparseCore 0:
  141.7 70.1 reduce-scatter.1
where the time goes:
time: 237 us; the launch traced here: 236 us
  blocking collectives  73.8 us (31%)
  waiting for transfers between devices  73.4 us (31%)
  starting transfers between devices  28 us (12%)
  local copies, waits for them, and re-layouts  27.8 us (12%)
  matrix products  16 us (7%)
  between operations  14.1 us (6%)
  other arithmetic  3.23 us (1%)
    all_gather x1, blocking collectives, on_device(): tokens_full = lax.all_gather(features, 'shard', axis=2, tiled=True)[0]  73.8 us
    reduce_scatter x1, waiting for transfers between devices, on_device(): lax.psum_scatter(terms, 'shard', scatter_dimension=1, tiled=True)  61.6 us
    all_to_all x1, starting transfers between devices, on_device(): lax.all_to_all(weights_here, 'path', split_axis=0, concat_axis=0, tiled=T...  14.9 us
    all_to_all x1, starting transfers between devices, on_device(): lax.all_to_all(chosen, 'path', split_axis=0, concat_axis=0, tiled=True)  13.1 us
    all_to_all x1, waiting for transfers between devices, on_device(): lax.all_to_all(chosen, 'path', split_axis=0, concat_axis=0, tiled=True)  11.1 us
    unnamed x14, local copies, waits for them, and re-layouts  8.57 us
    all_to_all x2, local copies, waits for them, and re-layouts, on_device(): lax.all_to_all(weights_here, 'path', split_axis=0, concat_axis=0, tiled=T...  7.88 us
    all_to_all x1, local copies, waits for them, and re-layouts, on_device(): lax.all_to_all(chosen, 'path', split_axis=0, concat_axis=0, tiled=True)  4.95 us
  transfers between devices with their start and end apart: 3, of which 3 were waited for; matrix products, arithmetic and copies ran while one was open for 10% of the time, Pallas kernels for 0%

commit v1 on v0

v1 whole, which is shorter than its diff:
```python
import functools

import jax
import jax.numpy as jnp
from jax import lax
from jax.experimental import pallas as pl
from jax.experimental.pallas import tpu as pltpu
from jax.sharding import Mesh, PartitionSpec as P

D = 768
FF_HERE = 1536
MODULES = 16
COLS_A = 1024
COLS_B = FF_HERE - COLS_A
BLOCK = 256
PLANE = ("y", "x", "core")
PATH = ("y", "zh", "x", "core")

outer_momentum = 0.9
outer_rate = 0.7

bf16 = jnp.bfloat16
f32 = jnp.float32
i32 = jnp.int32


def silu_slope(pre):
    sigmoid_part = jax.nn.sigmoid(pre)
    return sigmoid_part * (1.0 + pre * (1.0 - sigmoid_part))


def mm(a, b):
    return jnp.dot(a, b, preferred_element_type=f32)


def mm_nt(a, b):
    return lax.dot_general(a, b, (((1,), (1,)), ((), ())), preferred_element_type=f32)


def iota(shape, axis):
    return lax.broadcasted_iota(i32, shape, axis)


def sixth(i):
    return (i * 10923) >> 16


def hot(mask):
    return jnp.where(mask, 1.0, 0.0).astype(bf16)


def message_parts(i):
    v = sixth(i)
    return v >> 2, v & 3, i - 6 * v


def natural_row(peer, zh, r):
    return (((((peer >> 3) * 4) + zh) << 3) + (peer & 7)) * 6 + r


def path_of(peer, zh):
    return ((((peer >> 3) * 4) + zh) << 3) + (peer & 7)


def call(kernel, ins, in_specs, out_shapes, out_specs, grid, zh, scratch=(), flops=0, aliases=None):
    return pl.pallas_call(
        kernel,
        grid_spec=pltpu.PrefetchScalarGridSpec(
            num_scalar_prefetch=1,
            grid=grid,
            in_specs=in_specs,
            out_specs=out_specs,
            scratch_shapes=list(scratch),
        ),
        out_shape=out_shapes,
        input_output_aliases=aliases or {},
        cost_estimate=pl.CostEstimate(flops=flops, bytes_accessed=4 << 20, transcendentals=0),
        compiler_params=pltpu.CompilerParams(vmem_limit_bytes=40 << 20),
    )(zh, *ins)


def cols(rows, first=0):
    return pl.BlockSpec((rows, BLOCK), lambda j, z: (0, j + first))


def whole(rows, width):
    return pl.BlockSpec((rows, width), lambda j, z: (0, 0))


def shape(rows, width, kind):
    return jax.ShapeDtypeStruct((rows, width), kind)


FLOPS = 2 * 768 * 768


def strips_kernel(z, *refs):
    for k in range(4):
        refs[4 + k][...] = refs[k][...].reshape(192, COLS_B)


def strips(weights, zh):
    view = weights.reshape(4, 4, 48, FF_HERE)
    specs = [
        pl.BlockSpec((4, 1, 48, COLS_B), functools.partial(lambda j, z, d: (0, (z[0] + d) & 3, 0, COLS_A // COLS_B), d=d))
        for d in range(4)
    ]
    return call(
        strips_kernel, [view] * 4, specs, [shape(192, COLS_B, bf16)] * 4, [whole(192, COLS_B)] * 4, (1,), zh, flops=FLOPS * 256
    )


def pack_a_kernel(z, w, out, perm):
    @pl.when(pl.program_id(0) == 0)
    def _():
        i = iota((1, 768), 1)
        u = sixth(i)
        peer = ((u >> 5) << 3) + (u & 7)
        target = peer * 24 + ((u >> 3) & 3) * 6 + i - 6 * u
        perm[...] = hot(iota((768, 768), 0) == target)

    out[...] = mm(perm[...], w[...]).astype(bf16)


def pack_a(weights, zh):
    return call(
        pack_a_kernel, [weights], [cols(768)], shape(768, COLS_A, bf16), cols(768), (COLS_A // BLOCK,), zh,
        [pltpu.VMEM((768, 768), bf16)], FLOPS * COLS_A,
    )


def pack_b_kernel(z, b0, b1, b2, b3, out, perm):
    @pl.when(pl.program_id(0) == 0)
    def _():
        k = iota((1, 768), 1)
        v = sixth(k)
        target = (v & 31) * 24 + (v >> 5) * 6 + k - 6 * v
        perm[...] = hot(iota((768, 768), 0) == target)

    out[...] = mm(perm[...], jnp.concatenate([b0[...], b1[...], b2[...], b3[...]], axis=0)).astype(bf16)


def pack_b(blocks, zh):
    return call(
        pack_b_kernel, blocks, [cols(192)] * 4, shape(768, COLS_B, bf16), cols(768), (COLS_B // BLOCK,), zh,
        [pltpu.VMEM((768, 768), bf16)], FLOPS * COLS_B,
    )


def module_rows(mods, rows):
    return hot((iota((rows, 128), 0) & 15) == mods[...])


def sum_a_kernel(z, mods, msg, o0, o1, o2, o3, pick):
    zh = z[0]

    @pl.when(pl.program_id(0) == 0)
    def _():
        peer, q, r = message_parts(iota((1, 768), 1))
        lanes = mm(module_rows(mods, 96), hot(iota((128, 768), 0) == path_of(peer, zh)))
        lanes = jnp.where((iota((96, 768), 0) >> 4) == r, lanes, 0.0)
        for d in range(4):
            pick[d * 96 : (d + 1) * 96, :] = jnp.where(q == ((zh + d) & 3), lanes, 0.0).astype(bf16)

    sums = mm(pick[...], msg[...])
    o0[...] = sums[0:96]
    o1[...] = sums[96:192].astype(bf16)
    o2[...] = sums[192:288].astype(bf16)
    o3[...] = sums[288:384].astype(bf16)


def sum_a(mods, msg, zh):
    return call(
        sum_a_kernel, [mods, msg], [whole(1, 128), cols(768)],
        [shape(96, COLS_A, f32)] + [shape(96, COLS_A, bf16)] * 3, [cols(96)] * 4, (COLS_A // BLOCK,), zh,
        [pltpu.VMEM((384, 768), bf16)], FLOPS * COLS_A // 2,
    )


def outer_step(summed, counts, params, moment):
    pseudo = params - summed / counts
    moment_new = outer_momentum * moment + pseudo
    params_new = params - outer_rate * (pseudo + outer_momentum * moment_new)
    return params_new, moment_new


def count_rows(mods):
    return jnp.sum(module_rows(mods, 96).astype(f32), axis=1, keepdims=True)


def step_a_kernel(z, mods, s0, s1, s2, s3, params, moment, new_params, new_moment, rounded):
    summed = s0[...] + s1[...].astype(f32) + s2[...].astype(f32) + s3[...].astype(f32)
    p, m = outer_step(summed, count_rows(mods), params[...], moment[...])
    new_params[...] = p
    new_moment[...] = m
    rounded[...] = p.astype(bf16)


def step_a(mods, sums, params, moment, zh):
    return call(
        step_a_kernel, [mods, *sums, params, moment], [whole(1, 128)] + [cols(96)] * 6,
        [shape(96, COLS_A, f32)] * 2 + [shape(96, COLS_A, bf16)], [cols(96)] * 3, (COLS_A // BLOCK,), zh, flops=FLOPS * 512,
    )


def step_b_kernel(z, mods, msg, params, moment, new_params, new_moment, out, pick, give):
    zh = z[0]

    @pl.when(pl.program_id(0) == 0)
    def _():
        peer, q, r = message_parts(iota((1, 768), 1))
        lanes = mm(module_rows(mods, 96), hot(iota((128, 768), 0) == path_of(peer, (zh - q) & 3)))
        pick[...] = jnp.where((iota((96, 768), 0) >> 4) == r, lanes, 0.0).astype(bf16)
        peer, q, r = message_parts(iota((768, 128), 0))
        rows = mm_nt(hot(path_of(peer, q) == iota((768, 128), 1)), module_rows(mods, 96))
        r = message_parts(iota((768, 96), 0))[2]
        give[...] = jnp.where(r == (iota((768, 96), 1) >> 4), rows, 0.0).astype(bf16)

    p, m = outer_step(mm(pick[...], msg[...]), count_rows(mods), params[...], moment[...])
    new_params[...] = p
    new_moment[...] = m
    out[...] = mm(give[...], p.astype(bf16)).astype(bf16)


def step_b(mods, msg, params, moment, zh):
    first = COLS_A // BLOCK
    return call(
        step_b_kernel, [mods, msg, params, moment], [whole(1, 128), cols(768), cols(96, first), cols(96, first)],
        [shape(96, COLS_B, f32)] * 2 + [shape(768, COLS_B, bf16)], [cols(96)] * 2 + [cols(768)], (COLS_B // BLOCK,), zh,
        [pltpu.VMEM((96, 768), bf16), pltpu.VMEM((768, 96), bf16)], FLOPS * COLS_B,
    )


def give_a_kernel(z, mods, b0, b1, b2, b3, out, give):
    zh = z[0]

    @pl.when(pl.program_id(0) == 0)
    def _():
        peer = message_parts(iota((768, 128), 0))[0]
        rows = mm_nt(hot(path_of(peer, zh) == iota((768, 128), 1)), module_rows(mods, 384))
        _, q, r = message_parts(iota((768, 384), 0))
        want = q * 6 + r
        give[...] = jnp.where(want == (iota((768, 384), 1) >> 4), rows, 0.0).astype(bf16)

    out[...] = mm(give[...], jnp.concatenate([b0[...], b1[...], b2[...], b3[...]], axis=0)).astype(bf16)


def give_a(mods, blocks, zh):
    return call(
        give_a_kernel, [mods, *blocks], [whole(1, 128)] + [cols(96)] * 4, shape(768, COLS_A, bf16), cols(768),
        (COLS_A // BLOCK,), zh, [pltpu.VMEM((768, 384), bf16)], FLOPS * COLS_A,
    )


def split_b_kernel(z, msg, o0, o1, o2, o3, perm):
    zh = z[0]

    @pl.when(pl.program_id(0) == 0)
    def _():
        peer, q, r = message_parts(iota((1, 768), 1))
        target = ((q - zh) & 3) * 192 + peer * 6 + r
        perm[...] = hot(iota((768, 768), 0) == target)

    rows = mm(perm[...], msg[...]).astype(bf16)
    for d, ref in enumerate((o0, o1, o2, o3)):
        ref[...] = rows[d * 192 : (d + 1) * 192]


def split_b(msg, zh):
    return call(
        split_b_kernel, [msg], [cols(768)], [shape(192, COLS_B, bf16)] * 4, [cols(192)] * 4, (COLS_B // BLOCK,), zh,
        [pltpu.VMEM((768, 768), bf16)], FLOPS * COLS_B,
    )


def out_spec(first):
    return pl.BlockSpec((4, 4, 48, BLOCK), lambda j, z: (0, 0, 0, j + first))


OUT = jax.ShapeDtypeStruct((4, 4, 48, FF_HERE), bf16)


def final_a_kernel(z, msg, out, perm):
    zh = z[0]

    @pl.when(pl.program_id(0) == 0)
    def _():
        peer, q, r = message_parts(iota((1, 768), 1))
        perm[...] = hot(iota((768, 768), 0) == natural_row(peer, (zh - q) & 3, r))

    out[...] = mm(perm[...], msg[...]).astype(bf16).reshape(4, 4, 48, BLOCK)


def final_a(msg, zh):
    return call(
        final_a_kernel, [msg], [cols(768)], OUT, out_spec(0), (COLS_A // BLOCK,), zh,
        [pltpu.VMEM((768, 768), bf16)], FLOPS * COLS_A,
    )


def final_b_kernel(z, b0, b1, b2, b3, old, out):
    for d, ref in enumerate((b0, b1, b2, b3)):
        out[:, pl.ds((z[0] - d) & 3, 1), :, :] = ref[...].reshape(4, 1, 48, BLOCK)


def final_b(blocks, old, zh):
    return call(
        final_b_kernel, [*blocks, old], [cols(192)] * 4 + [pl.BlockSpec(memory_space=pl.ANY)], OUT,
        out_spec(COLS_A // BLOCK), (COLS_B // BLOCK,), zh, flops=FLOPS * 256, aliases={5: 0},
    )


def shift_z(block, d):
    return lax.ppermute(block, "zh", [(i, (i + d) % 4) for i in range(4)])


def shift_all(blocks):
    moved = {d: shift_z(blocks[d], d) for d in (2, 1, 3)}
    return [blocks[0]] + [moved[d] for d in (1, 2, 3)]


def plane_exchange(rows):
    blocks = rows.reshape(32, 24, rows.shape[-1])
    return lax.all_to_all(blocks, PLANE, 0, 0, tiled=True).reshape(rows.shape)


def after(value, earlier):
    return lax.optimization_barrier((value, earlier))


def on_device(features, path_weights, cotangent, path_module, outer_params, outer_moment):
    multiplier = D ** (-0.5)
    weights = path_weights[0]
    zh = lax.axis_index("zh").reshape(1)
    first = lax.axis_index("shard") == 0
    mods = path_module.reshape(1, 128)
    params = outer_params.transpose(1, 0, 2).reshape(96, FF_HERE)
    moment = outer_moment.transpose(1, 0, 2).reshape(96, FF_HERE)

    swap = [(0, 1), (1, 0)]
    other = lax.ppermute(features[0], "shard", swap)

    got_b = shift_all(strips(weights, zh))
    in_a = plane_exchange(pack_a(weights, zh))
    out_b, in_a = after(pack_b(got_b, zh), in_a)
    in_b = plane_exchange(out_b)

    sums_a = shift_all(sum_a(mods, in_a, zh))
    params_a, moment_a, mine_a = step_a(mods, sums_a, params, moment, zh)
    params_b, moment_b, back_out_b = step_b(mods, in_b, params, moment, zh)
    back_b = plane_exchange(back_out_b)

    every_a = shift_all([mine_a] * 4)
    back_out_a, back_b = after(give_a(mods, every_a, zh), back_b)
    back_a = plane_exchange(back_out_a)

    home_b = shift_all(split_b(back_b, zh))
    synced = final_b(home_b, final_a(back_a, zh), zh).reshape(1, 768, FF_HERE)

    params_new = jnp.concatenate([params_a, params_b], axis=1)
    moment_new = jnp.concatenate([moment_a, moment_b], axis=1)
    params_new = params_new.reshape(6, MODULES, FF_HERE).transpose(1, 0, 2)
    moment_new = moment_new.reshape(6, MODULES, FF_HERE).transpose(1, 0, 2)

    tokens = jnp.concatenate(
        [jnp.where(first, features[0], other), jnp.where(first, other, features[0])], axis=1
    )
    pre = mm(tokens, weights) * multiplier
    delta = (cotangent[0].astype(f32) * silu_slope(pre)).astype(bf16)
    grad_w = lax.dot_general(tokens, delta, (((0,), (0,)), ((), ())), preferred_element_type=f32)
    grad_w = (grad_w * multiplier).astype(bf16)
    terms = mm_nt(delta, weights) * multiplier
    half = D // 2
    give = jnp.where(first, terms[:, half:], terms[:, :half]).astype(bf16)
    keep = jnp.where(first, terms[:, :half], terms[:, half:])
    grad_in = (keep + lax.ppermute(give, "shard", swap).astype(f32)).astype(bf16)
    return (synced, params_new, moment_new, grad_w[None], grad_in[None])


def solution(mesh):
    fine = Mesh(mesh.devices.reshape(4, 4, 4, 2, 2), ("y", "zh", "x", "core", "shard"))
    wide = P(PATH, None, "shard")
    state = P(None, PATH, "shard")
    return jax.shard_map(
        on_device,
        mesh=fine,
        in_specs=(wide, wide, wide, P(), state, state),
        out_specs=(wide, state, state, wide, wide),
        check_vma=False,
    )
```

time: 237 us -> 162 us (0.68)
  blocking collectives: 73.8 us -> 0 us
  starting transfers between devices: 28 us -> 63.6 us
  waiting for transfers between devices: 73.4 us -> 49.1 us
  Pallas kernels: 0 us -> 21.8 us
  local copies, waits for them, and re-layouts: 27.8 us -> 9.09 us
  between operations: 14.1 us -> 0.89 us
  matrix products: 16 us -> 10.8 us
    all_gather x1 -> x0, blocking collectives: 73.8 us -> none  [on_device(): tokens_full = lax.all_gather(features, 'shard', axis=2, tiled=True)[0]]
    reduce_scatter x1 -> x0, waiting for transfers between devices: 61.6 us -> none  [on_device(): lax.psum_scatter(terms, 'shard', scatter_dimension=1, tiled=True)]
    ppermute x0 -> x14, waiting for transfers between devices: none -> 42.7 us  [the longest x12 32 us: shift_z(): return lax.ppermute(block, 'zh', [(i, (i + d) % 4) for i in range(4)])]
    ppermute x0 -> x14, starting transfers between devices: none -> 36.7 us  [the longest x12 32 us: shift_z(): return lax.ppermute(block, 'zh', [(i, (i + d) % 4) for i in range(4)])]
    pallas_call x0 -> x10, Pallas kernels: none -> 21.8 us  [call(): pl.pallas_call(kernel, grid_spec=pltpu.PrefetchScalarGridSpec(num_scalar_...]
    all_to_all x3 -> x0, local copies, waits for them, and re-layouts: 12.8 us -> none  [the longest x2 7.88 us: on_device(): lax.all_to_all(weights_here, 'path', split_axis=0, concat_axis=0, tiled=T...]
    all_to_all x2 -> x4, waiting for transfers between devices: 11.8 us -> 6.44 us  [plane_exchange(): return lax.all_to_all(blocks, PLANE, 0, 0, tiled=True).reshape(rows.shape)]
    dot_general x5 -> x3, matrix products: 16 us -> 10.8 us  [the longest x1 5.01 us: mm(): return jnp.dot(a, b, preferred_element_type=f32)]
  transfers between devices with their start and end apart: 3 -> 18, of which waited for: 3 -> 11; matrix products, arithmetic and copies ran while one was open for 10% -> 9% of each run, Pallas kernels for 0% -> 12%
where the time goes in v1:
time: 162 us; the launch traced here: 159 us
  starting transfers between devices  63.6 us (39%)
  waiting for transfers between devices  49.1 us (30%)
  Pallas kernels  21.8 us (13%)
  matrix products  10.8 us (7%)
  local copies, waits for them, and re-layouts  9.09 us (6%)
  other arithmetic  3.97 us (2%)
    ppermute x12, waiting for transfers between devices, shift_z(): return lax.ppermute(block, 'zh', [(i, (i + d) % 4) for i in range(4)])  32 us
    ppermute x12, starting transfers between devices, shift_z(): return lax.ppermute(block, 'zh', [(i, (i + d) % 4) for i in range(4)])  32 us
    all_to_all x4, starting transfers between devices, plane_exchange(): return lax.all_to_all(blocks, PLANE, 0, 0, tiled=True).reshape(rows.shape)  26.9 us
    pallas_call x10, Pallas kernels, call(): pl.pallas_call(kernel, grid_spec=pltpu.PrefetchScalarGridSpec(num_scalar_...  21.8 us
    unnamed x40, local copies, waits for them, and re-layouts  9.09 us
    ppermute x1, waiting for transfers between devices, on_device(): lax.ppermute(give, 'shard', swap).astype(f32)  8.24 us
    all_to_all x4, waiting for transfers between devices, plane_exchange(): return lax.all_to_all(blocks, PLANE, 0, 0, tiled=True).reshape(rows.shape)  6.44 us
    dot_general x1, matrix products, mm(): return jnp.dot(a, b, preferred_element_type=f32)  5.01 us
  transfers between devices with their start and end apart: 18, of which 11 were waited for; matrix products, arithmetic and copies ran while one was open for 9% of the time, Pallas kernels for 12%

profile of v1, /device:TPU:32, one launch (start us, length us, event | category | flops | bytes accessed | tf_op | source)
XLA Modules:
  0.0 159.3 jit_solution(7301883943353462582)
XLA Ops:
  2.3 2.4 %shard_map.103 = bf16[768,1024]{1,0:T(8,128)(2,1)S(1)} custom-call(s32[1]{0:T(128)} %bitcast.z, bf16[768,1536]{1,0:T(8,128)(2,1)S(1)} %bitcast.41), custom_call_target="tpu_custom_call" | custom-call | flops 1207959552 | bytes 4194304 | tf_op jit(solution)/shard_map/pallas_call | solution.py:66
  5.9 7.6 %all-to-all-start = ((bf16[32,24,1024]{2,1,0:T(8,128)(2,1)}), bf16[32,24,1024]{2,1,0:T(8,128)(2,1)}, u32[]{:S(2)}, u32[]{:S(2)}) async-start(bf16[32,24,1024]{2,1,0:T(8,128)(2,1)} %bitcast.47), calls=%async_computation | async-start | bytes 3145728 | tf_op jit(solution)/shard_map/all_to_all | solution.py:324
  13.5 3.4 %collective-permute-start = (bf16[192,512]{1,0:T(8,128)(2,1)S(1)}, bf16[192,512]{1,0:T(8,128)(2,1)S(1)}, u32[]{:S(2)}, u32[]{:S(2)}) collective-permute-start(bf16[192,512]{1,0:T(8,128)(2,1)S(1)} %get-tuple-element.28), channel_id=1, source_target_pairs={{0,16},{16,32},{32,48},{48,0},{1,17},{17,33},{33,49},{49,1},{2,18}... | collective-permute-start | bytes 589832 | tf_op jit(solution)/shard_map/ppermute | solution.py:314
  16.9 4.5 %collective-permute-start.1 = (bf16[192,512]{1,0:T(8,128)(2,1)S(1)}, bf16[192,512]{1,0:T(8,128)(2,1)S(1)}, u32[]{:S(2)}, u32[]{:S(2)}) collective-permute-start(bf16[192,512]{1,0:T(8,128)(2,1)S(1)} %get-tuple-element.29), channel_id=1, source_target_pairs={{0,32},{16,48},{32,0},{48,16},{1,33},{17,49},{33,1},{49,17},{2,34}... | collective-permute-start | bytes 589832 | tf_op jit(solution)/shard_map/ppermute | solution.py:314
  21.4 2.7 %collective-permute-start.2 = (bf16[192,512]{1,0:T(8,128)(2,1)S(1)}, bf16[192,512]{1,0:T(8,128)(2,1)S(1)}, u32[]{:S(2)}, u32[]{:S(2)}) collective-permute-start(bf16[192,512]{1,0:T(8,128)(2,1)S(1)} %get-tuple-element.30), channel_id=1, source_target_pairs={{0,48},{16,0},{32,16},{48,32},{1,49},{17,1},{33,17},{49,33},{2,50}... | collective-permute-start | bytes 589832 | tf_op jit(solution)/shard_map/ppermute | solution.py:314
  24.1 10.3 %collective-permute-done.b1 = bf16[192,512]{1,0:T(8,128)(2,1)S(1)} collective-permute-done((bf16[192,512]{1,0:T(8,128)(2,1)S(1)}, bf16[192,512]{1,0:T(8,128)(2,1)S(1)}, u32[]{:S(2)}, u32[]{:S(2)}) %collective-permute-start) | collective-permute-done | bytes 196640 | tf_op jit(solution)/shard_map/ppermute | solution.py:314
  34.3 1.8 %collective-permute-done.2.b3 = bf16[192,512]{1,0:T(8,128)(2,1)S(1)} collective-permute-done((bf16[192,512]{1,0:T(8,128)(2,1)S(1)}, bf16[192,512]{1,0:T(8,128)(2,1)S(1)}, u32[]{:S(2)}, u32[]{:S(2)}) %collective-permute-start.2) | collective-permute-done | bytes 196640 | tf_op jit(solution)/shard_map/ppermute | solution.py:314
  36.1 2.0 %shard_map.102 = bf16[768,512]{1,0:T(8,128)(2,1)} custom-call(s32[1]{0:T(128)} %bitcast.z, bf16[192,512]{1,0:T(8,128)(2,1)S(1)} %get-tuple-element.27.b0, bf16[192,512]{1,0:T(8,128)(2,1)S(1)} %collective-permute-done.b1, bf16[192,512]{1,0:T(8,128)(2,1)S(1)} %collective-permute-done.1.b2, bf16[192,512]{1,0:T(8,128)(2,1)S(1)} %collective-permute-done.2.b3), custom_call_target="tpu_custom_call" | custom-call | flops 603979776 | bytes 4194304 | tf_op jit(solution)/shard_map/pallas_call | solution.py:66
  38.1 7.2 %all-to-all-start.1 = ((bf16[32,24,512]{2,1,0:T(8,128)(2,1)}), bf16[32,24,512]{2,1,0:T(8,128)(2,1)S(1)}, u32[]{:S(2)}, u32[]{:S(2)}) async-start(bf16[32,24,512]{2,1,0:T(8,128)(2,1)} %bitcast.10), calls=%async_computation.1 | async-start | bytes 1572864 | tf_op jit(solution)/shard_map/all_to_all | solution.py:324
  45.4 4.6 %collective-permute-start.12 = (bf16[512,384]{1,0:T(8,128)(2,1)S(1)}, bf16[512,384]{1,0:T(8,128)(2,1)}, u32[]{:S(2)}, u32[]{:S(2)}) collective-permute-start(bf16[512,384]{1,0:T(8,128)(2,1)S(1)} %bitcast.62), channel_id=1, source_target_pairs={{0,1},{1,0},{2,3},{3,2},{4,5},{5,4},{6,7},{7,6},{8,9},{9,8},{10,11... | collective-permute-start | bytes 1179656 | tf_op jit(solution)/shard_map/ppermute | solution.py:341
  50.0 3.4 %shard_map.104 = (f32[96,1024]{1,0:T(8,128)S(1)}, bf16[96,1024]{1,0:T(8,128)(2,1)S(1)}, bf16[96,1024]{1,0:T(8,128)(2,1)S(1)}, bf16[96,1024]{1,0:T(8,128)(2,1)S(1)}) custom-call(s32[1]{0:T(128)} %bitcast.z, s32[1,128]{1,0:T(1,128)S(1)} %bitcast.55, bf16[768,1024]{1,0:T(8,128)(2,1)} %bitcast.5.msg), custom_call_target="tpu_custom_call" | custom-call | flops 603979776 | bytes 4194304 | tf_op jit(solution)/shard_map/pallas_call | solution.py:66
  55.1 4.3 %collective-permute-start.4 = (bf16[96,1024]{1,0:T(8,128)(2,1)S(1)}, bf16[96,1024]{1,0:T(8,128)(2,1)S(1)}, u32[]{:S(2)}, u32[]{:S(2)}) collective-permute-start(bf16[96,1024]{1,0:T(8,128)(2,1)S(1)} %get-tuple-element.34), channel_id=1, source_target_pairs={{0,32},{16,48},{32,0},{48,16},{1,33},{17,49},{33,1},{49,17},{2,34}... | collective-permute-start | bytes 589832 | tf_op jit(solution)/shard_map/ppermute | solution.py:314
  59.4 2.5 %collective-permute-start.5 = (bf16[96,1024]{1,0:T(8,128)(2,1)S(1)}, bf16[96,1024]{1,0:T(8,128)(2,1)S(1)}, u32[]{:S(2)}, u32[]{:S(2)}) collective-permute-start(bf16[96,1024]{1,0:T(8,128)(2,1)S(1)} %get-tuple-element.35), channel_id=1, source_target_pairs={{0,48},{16,0},{32,16},{48,32},{1,49},{17,1},{33,17},{49,33},{2,50}... | collective-permute-start | bytes 589832 | tf_op jit(solution)/shard_map/ppermute | solution.py:314
  61.9 2.4 %collective-permute-done.12 = bf16[512,384]{1,0:T(8,128)(2,1)} collective-permute-done((bf16[512,384]{1,0:T(8,128)(2,1)S(1)}, bf16[512,384]{1,0:T(8,128)(2,1)}, u32[]{:S(2)}, u32[]{:S(2)}) %collective-permute-start.12) | collective-permute-done | bytes 393248 | tf_op jit(solution)/shard_map/ppermute | solution.py:341
  64.3 1.9 %broadcast_select_fusion.1 = (bf16[512,384]{1,0:T(8,128)(2,1)}, bf16[512,384]{1,0:T(8,128)(2,1)}) fusion(bf16[512,384]{1,0:T(8,128)(2,1)} %collective-permute-done.12, pred[]{:T(512)S(6)} %eq.3, bf16[1,512,384]{2,1,0:T(8,128)(2,1)S(1)} %copy-done.16), kind=kLoop, calls=%fused_computation.13 | loop fusion | flops 393216 | bytes 1572865 | tf_op jit(solution)/shard_map/jit(_where)/select_n | solution.py:366
  66.2 10.5 %collective-permute-done.4.s2 = bf16[96,1024]{1,0:T(8,128)(2,1)S(1)} collective-permute-done((bf16[96,1024]{1,0:T(8,128)(2,1)S(1)}, bf16[96,1024]{1,0:T(8,128)(2,1)S(1)}, u32[]{:S(2)}, u32[]{:S(2)}) %collective-permute-start.4) | collective-permute-done | bytes 196640 | tf_op jit(solution)/shard_map/ppermute | solution.py:314
  77.7 1.8 %shard_map.105 = (f32[96,1024]{1,0:T(8,128)S(1)}, f32[96,1024]{1,0:T(8,128)S(1)}, bf16[96,1024]{1,0:T(8,128)(2,1)}) custom-call(s32[1]{0:T(128)} %bitcast.z, s32[1,128]{1,0:T(1,128)S(1)} %bitcast.56, f32[96,1024]{1,0:T(8,128)S(1)} %get-tuple-element.32.s0, bf16[96,1024]{1,0:T(8,128)(2,1)S(1)} %collective-permute-done.3.s1, ...), custom_call_target="tpu_custom_call" | custom-call | flops 603979776 | bytes 4194304 | tf_op jit(solution)/shard_map/pallas_call | solution.py:66
  80.3 3.2 %collective-permute-start.6 = (bf16[96,1024]{1,0:T(8,128)(2,1)}, bf16[96,1024]{1,0:T(8,128)(2,1)}, u32[]{:S(2)}, u32[]{:S(2)}) collective-permute-start(bf16[96,1024]{1,0:T(8,128)(2,1)} %get-tuple-element.36.b0), channel_id=1, source_target_pairs={{0,16},{16,32},{32,48},{48,0},{1,17},{17,33},{33,49},{49,1},{2,18}... | collective-permute-start | bytes 589832 | tf_op jit(solution)/shard_map/ppermute | solution.py:314
  83.5 2.1 %collective-permute-start.7 = (bf16[96,1024]{1,0:T(8,128)(2,1)}, bf16[96,1024]{1,0:T(8,128)(2,1)}, u32[]{:S(2)}, u32[]{:S(2)}) collective-permute-start(bf16[96,1024]{1,0:T(8,128)(2,1)} %get-tuple-element.36.b0), channel_id=1, source_target_pairs={{0,32},{16,48},{32,0},{48,16},{1,33},{17,49},{33,1},{49,17},{2,34}... | collective-permute-start | bytes 589832 | tf_op jit(solution)/shard_map/ppermute | solution.py:314
  85.6 3.1 %collective-permute-start.8 = (bf16[96,1024]{1,0:T(8,128)(2,1)}, bf16[96,1024]{1,0:T(8,128)(2,1)}, u32[]{:S(2)}, u32[]{:S(2)}) collective-permute-start(bf16[96,1024]{1,0:T(8,128)(2,1)} %get-tuple-element.36.b0), channel_id=1, source_target_pairs={{0,48},{16,0},{32,16},{48,32},{1,49},{17,1},{33,17},{49,33},{2,50}... | collective-permute-start | bytes 589832 | tf_op jit(solution)/shard_map/ppermute | solution.py:314
  94.8 7.4 %all-to-all-start.2 = ((bf16[32,24,512]{2,1,0:T(8,128)(2,1)}), bf16[32,24,512]{2,1,0:T(8,128)(2,1)S(1)}, u32[]{:S(2)}, u32[]{:S(2)}) async-start(bf16[32,24,512]{2,1,0:T(8,128)(2,1)} %bitcast.50), calls=%async_computation.2 | async-start | bytes 1572864 | tf_op jit(solution)/shard_map/all_to_all | solution.py:324
  102.2 5.0 %fusion = bf16[512,1536]{1,0:T(8,128)(2,1)} fusion(bf16[1,512,1536]{2,1,0:T(8,128)(2,1)} %param.8, bf16[512,384]{1,0:T(8,128)(2,1)} %get-tuple-element.50, bf16[512,384]{1,0:T(8,128)(2,1)} %get-tuple-element.49, bf16[1,768,1536]{2,1,0:T(8,128)(2,1)S(1)} %copy-done.1), kind=kOutput, calls=%fused_computation.3 | convolution fusion | flops 1218183168 | bytes 6291456 | tf_op jit(solution)/shard_map/dot_general | solution.py:33
  107.2 3.4 %shard_map.106 = bf16[768,1024]{1,0:T(8,128)(2,1)S(1)} custom-call(s32[1]{0:T(128)} %bitcast.z, s32[1,128]{1,0:T(1,128)S(1)} %bitcast.58, bf16[96,1024]{1,0:T(8,128)(2,1)} %get-tuple-element.36.b0, bf16[96,1024]{1,0:T(8,128)(2,1)} %collective-permute-done.6.b1, bf16[96,1024]{1,0:T(8,128)(2,1)} %collective-permute-done.7.b2, ...), custom_call_target="tpu_custom_call" | custom-call | flops 1207959552 | bytes 4194304 | tf_op jit(solution)/shard_map/pallas_call | solution.py:66
  111.7 4.8 %all-to-all-done.2 = bf16[32,24,512]{2,1,0:T(8,128)(2,1)S(1)} async-done(((bf16[32,24,512]{2,1,0:T(8,128)(2,1)}), bf16[32,24,512]{2,1,0:T(8,128)(2,1)S(1)}, u32[]{:S(2)}, u32[]{:S(2)}) %all-to-all-start.2) | async-done | bytes 786464 | tf_op jit(solution)/shard_map/all_to_all | solution.py:324
  116.5 4.7 %all-to-all-start.3 = ((bf16[32,24,1024]{2,1,0:T(8,128)(2,1)}), bf16[32,24,1024]{2,1,0:T(8,128)(2,1)}, u32[]{:S(2)}, u32[]{:S(2)}) async-start(bf16[32,24,1024]{2,1,0:T(8,128)(2,1)} %bitcast.46), calls=%async_computation.3 | async-start | bytes 3145728 | tf_op jit(solution)/shard_map/all_to_all | solution.py:324
  121.3 3.0 %convolution_multiply_fusion.1 = f32[512,768]{1,0:T(8,128)S(1)} fusion(bf16[512,1536]{1,0:T(8,128)(2,1)} %fusion, bf16[1,768,1536]{2,1,0:T(8,128)(2,1)S(1)} %copy-done.1), kind=kOutput, calls=%fused_computation.5 | convolution fusion | flops 1208352768 | bytes 5505024 | tf_op jit(solution)/shard_map/dot_general | solution.py:37
  124.4 2.8 %fusion.1 = bf16[1,768,1536]{2,1,0:T(8,128)(2,1)} fusion(bf16[512,1536]{1,0:T(8,128)(2,1)S(1)} %copy-done.19, bf16[512,384]{1,0:T(8,128)(2,1)S(1)} %copy-done.18, bf16[512,384]{1,0:T(8,128)(2,1)S(1)} %copy-done.17), kind=kOutput, calls=%fused_computation.4 | convolution fusion | flops 1211891712 | bytes 4718592 | tf_op jit(solution)/shard_map/dot_general | solution.py:370
  127.3 8.2 %collective-permute-done.13 = bf16[512,384]{1,0:T(8,128)(2,1)S(1)} collective-permute-done((bf16[512,384]{1,0:T(8,128)(2,1)S(1)}, bf16[512,384]{1,0:T(8,128)(2,1)S(1)}, u32[]{:S(2)}, u32[]{:S(2)}) %collective-permute-start.13) | collective-permute-done | bytes 393248 | tf_op jit(solution)/shard_map/ppermute | solution.py:376
  145.1 4.7 %shard_map.109.old = bf16[4,4,48,1536]{3,2,1,0:T(8,128)(2,1)} custom-call(s32[1]{0:T(128)} %bitcast.z, bf16[768,1024]{1,0:T(8,128)(2,1)} %bitcast.17.msg), custom_call_target="tpu_custom_call" | custom-call | flops 1207959552 | bytes 4194304 | tf_op jit(solution)/shard_map/pallas_call | solution.py:66
  149.8 1.8 %collective-permute-done.10.b2 = bf16[192,512]{1,0:T(8,128)(2,1)S(1)} collective-permute-done((bf16[192,512]{1,0:T(8,128)(2,1)S(1)}, bf16[192,512]{1,0:T(8,128)(2,1)S(1)}, u32[]{:S(2)}, u32[]{:S(2)}) %collective-permute-start.10) | collective-permute-done | bytes 196640 | tf_op jit(solution)/shard_map/ppermute | solution.py:314
  151.6 2.5 %collective-permute-done.11.b3 = bf16[192,512]{1,0:T(8,128)(2,1)S(1)} collective-permute-done((bf16[192,512]{1,0:T(8,128)(2,1)S(1)}, bf16[192,512]{1,0:T(8,128)(2,1)S(1)}, u32[]{:S(2)}, u32[]{:S(2)}) %collective-permute-start.11) | collective-permute-done | bytes 196640 | tf_op jit(solution)/shard_map/ppermute | solution.py:314
  154.2 4.1 %collective-permute-done.9.b1 = bf16[192,512]{1,0:T(8,128)(2,1)S(1)} collective-permute-done((bf16[192,512]{1,0:T(8,128)(2,1)S(1)}, bf16[192,512]{1,0:T(8,128)(2,1)S(1)}, u32[]{:S(2)}, u32[]{:S(2)}) %collective-permute-start.9) | collective-permute-done | bytes 196640 | tf_op jit(solution)/shard_map/ppermute | solution.py:314
  (61 shorter events, 24.2 us)
Async XLA Ops:
  0.6 1.7 %copy-start = (bf16[1,768,1536]{2,1,0:T(8,128)(2,1)S(1)}, bf16[1,768,1536]{2,1,0:T(8,128)(2,1)}, u32[]{:S(2)}) copy-start(bf16[1,768,1536]{2,1,0:T(8,128)(2,1)} %param.7) | copy-start | bytes 7077892
  4.7 1.1 copy-start.3
  5.9 7.6 %copy-start.1 = (bf16[1,768,1536]{2,1,0:T(8,128)(2,1)S(1)}, bf16[1,768,1536]{2,1,0:T(8,128)(2,1)}, u32[]{:S(2)}) copy-start(bf16[1,768,1536]{2,1,0:T(8,128)(2,1)} %param.7) | copy-start | bytes 7077892
  5.9 32.2 %all-to-all-start = ((bf16[32,24,1024]{2,1,0:T(8,128)(2,1)}), bf16[32,24,1024]{2,1,0:T(8,128)(2,1)}, u32[]{:S(2)}, u32[]{:S(2)}) async-start(bf16[32,24,1024]{2,1,0:T(8,128)(2,1)} %bitcast.47), calls=%async_computation | async-start | bytes 3145728 | tf_op jit(solution)/shard_map/all_to_all | solution.py:324
  13.5 31.8 %copy-start.16 = (bf16[1,512,384]{2,1,0:T(8,128)(2,1)S(1)}, bf16[1,512,384]{2,1,0:T(8,128)(2,1)}, u32[]{:S(2)}) copy-start(bf16[1,512,384]{2,1,0:T(8,128)(2,1)} %param.6) | copy-start | bytes 1179652
  13.5 36.5 %copy-start.15 = (s32[128,1]{0,1:T(1,128)S(1)}, s32[128,1]{0,1:T(1,128)}, u32[]{:S(2)}) copy-start(s32[128,1]{0,1:T(1,128)} %param.9) | copy-start | bytes 1540
  13.5 20.8 %collective-permute-start = (bf16[192,512]{1,0:T(8,128)(2,1)S(1)}, bf16[192,512]{1,0:T(8,128)(2,1)S(1)}, u32[]{:S(2)}, u32[]{:S(2)}) collective-permute-start(bf16[192,512]{1,0:T(8,128)(2,1)S(1)} %get-tuple-element.28), channel_id=1, source_target_pairs={{0,16},{16,32},{32,48},{48,0},{1,17},{17,33},{33,49},{49,1},{2,18}... | collective-permute-start | bytes 589832 | tf_op jit(solution)/shard_map/ppermute | solution.py:314
  16.9 17.4 %collective-permute-start.1 = (bf16[192,512]{1,0:T(8,128)(2,1)S(1)}, bf16[192,512]{1,0:T(8,128)(2,1)S(1)}, u32[]{:S(2)}, u32[]{:S(2)}) collective-permute-start(bf16[192,512]{1,0:T(8,128)(2,1)S(1)} %get-tuple-element.29), channel_id=1, source_target_pairs={{0,32},{16,48},{32,0},{48,16},{1,33},{17,49},{33,1},{49,17},{2,34}... | collective-permute-start | bytes 589832 | tf_op jit(solution)/shard_map/ppermute | solution.py:314
  21.4 14.7 %collective-permute-start.2 = (bf16[192,512]{1,0:T(8,128)(2,1)S(1)}, bf16[192,512]{1,0:T(8,128)(2,1)S(1)}, u32[]{:S(2)}, u32[]{:S(2)}) collective-permute-start(bf16[192,512]{1,0:T(8,128)(2,1)S(1)} %get-tuple-element.30), channel_id=1, source_target_pairs={{0,48},{16,0},{32,16},{48,32},{1,49},{17,1},{33,17},{49,33},{2,50}... | collective-permute-start | bytes 589832 | tf_op jit(solution)/shard_map/ppermute | solution.py:314
  38.1 50.6 %all-to-all-start.1 = ((bf16[32,24,512]{2,1,0:T(8,128)(2,1)}), bf16[32,24,512]{2,1,0:T(8,128)(2,1)S(1)}, u32[]{:S(2)}, u32[]{:S(2)}) async-start(bf16[32,24,512]{2,1,0:T(8,128)(2,1)} %bitcast.10), calls=%async_computation.1 | async-start | bytes 1572864 | tf_op jit(solution)/shard_map/all_to_all | solution.py:324
  45.4 18.9 %collective-permute-start.12 = (bf16[512,384]{1,0:T(8,128)(2,1)S(1)}, bf16[512,384]{1,0:T(8,128)(2,1)}, u32[]{:S(2)}, u32[]{:S(2)}) collective-permute-start(bf16[512,384]{1,0:T(8,128)(2,1)S(1)} %bitcast.62), channel_id=1, source_target_pairs={{0,1},{1,0},{2,3},{3,2},{4,5},{5,4},{6,7},{7,6},{8,9},{9,8},{10,11... | collective-permute-start | bytes 1179656 | tf_op jit(solution)/shard_map/ppermute | solution.py:341
  50.0 27.7 %copy-start.11 = (f32[16,6,1536]{2,0,1:T(8,128)S(1)}, f32[16,6,1536]{2,0,1:T(8,128)}, u32[]{:S(2)}) copy-start(f32[16,6,1536]{2,0,1:T(8,128)} %param.10) | copy-start | bytes 1769476
  50.0 27.7 %copy-start.13 = (f32[16,6,1536]{2,0,1:T(8,128)S(1)}, f32[16,6,1536]{2,0,1:T(8,128)}, u32[]{:S(2)}) copy-start(f32[16,6,1536]{2,0,1:T(8,128)} %param.11) | copy-start | bytes 1769476
  53.4 12.8 %collective-permute-start.3 = (bf16[96,1024]{1,0:T(8,128)(2,1)S(1)}, bf16[96,1024]{1,0:T(8,128)(2,1)S(1)}, u32[]{:S(2)}, u32[]{:S(2)}) collective-permute-start(bf16[96,1024]{1,0:T(8,128)(2,1)S(1)} %get-tuple-element.33), channel_id=1, source_target_pairs={{0,16},{16,32},{32,48},{48,0},{1,17},{17,33},{33,49},{49,1},{2,18}... | collective-permute-start | bytes 589832 | tf_op jit(solution)/shard_map/ppermute | solution.py:314
  55.1 21.7 %collective-permute-start.4 = (bf16[96,1024]{1,0:T(8,128)(2,1)S(1)}, bf16[96,1024]{1,0:T(8,128)(2,1)S(1)}, u32[]{:S(2)}, u32[]{:S(2)}) collective-permute-start(bf16[96,1024]{1,0:T(8,128)(2,1)S(1)} %get-tuple-element.34), channel_id=1, source_target_pairs={{0,32},{16,48},{32,0},{48,16},{1,33},{17,49},{33,1},{49,17},{2,34}... | collective-permute-start | bytes 589832 | tf_op jit(solution)/shard_map/ppermute | solution.py:314
  59.4 18.3 %collective-permute-start.5 = (bf16[96,1024]{1,0:T(8,128)(2,1)S(1)}, bf16[96,1024]{1,0:T(8,128)(2,1)S(1)}, u32[]{:S(2)}, u32[]{:S(2)}) collective-permute-start(bf16[96,1024]{1,0:T(8,128)(2,1)S(1)} %get-tuple-element.35), channel_id=1, source_target_pairs={{0,48},{16,0},{32,16},{48,32},{1,49},{17,1},{33,17},{49,33},{2,50}... | collective-permute-start | bytes 589832 | tf_op jit(solution)/shard_map/ppermute | solution.py:314
  80.3 26.9 %collective-permute-start.6 = (bf16[96,1024]{1,0:T(8,128)(2,1)}, bf16[96,1024]{1,0:T(8,128)(2,1)}, u32[]{:S(2)}, u32[]{:S(2)}) collective-permute-start(bf16[96,1024]{1,0:T(8,128)(2,1)} %get-tuple-element.36.b0), channel_id=1, source_target_pairs={{0,16},{16,32},{32,48},{48,0},{1,17},{17,33},{33,49},{49,1},{2,18}... | collective-permute-start | bytes 589832 | tf_op jit(solution)/shard_map/ppermute | solution.py:314
  83.5 23.7 %collective-permute-start.7 = (bf16[96,1024]{1,0:T(8,128)(2,1)}, bf16[96,1024]{1,0:T(8,128)(2,1)}, u32[]{:S(2)}, u32[]{:S(2)}) collective-permute-start(bf16[96,1024]{1,0:T(8,128)(2,1)} %get-tuple-element.36.b0), channel_id=1, source_target_pairs={{0,32},{16,48},{32,0},{48,16},{1,33},{17,49},{33,1},{49,17},{2,34}... | collective-permute-start | bytes 589832 | tf_op jit(solution)/shard_map/ppermute | solution.py:314
  85.6 21.6 %collective-permute-start.8 = (bf16[96,1024]{1,0:T(8,128)(2,1)}, bf16[96,1024]{1,0:T(8,128)(2,1)}, u32[]{:S(2)}, u32[]{:S(2)}) collective-permute-start(bf16[96,1024]{1,0:T(8,128)(2,1)} %get-tuple-element.36.b0), channel_id=1, source_target_pairs={{0,48},{16,0},{32,16},{48,32},{1,49},{17,1},{33,17},{49,33},{2,50}... | collective-permute-start | bytes 589832 | tf_op jit(solution)/shard_map/ppermute | solution.py:314
  94.8 21.8 %all-to-all-start.2 = ((bf16[32,24,512]{2,1,0:T(8,128)(2,1)}), bf16[32,24,512]{2,1,0:T(8,128)(2,1)S(1)}, u32[]{:S(2)}, u32[]{:S(2)}) async-start(bf16[32,24,512]{2,1,0:T(8,128)(2,1)} %bitcast.50), calls=%async_computation.2 | async-start | bytes 1572864 | tf_op jit(solution)/shard_map/all_to_all | solution.py:324
  110.6 1.1 copy-start.2
  116.5 28.6 %all-to-all-start.3 = ((bf16[32,24,1024]{2,1,0:T(8,128)(2,1)}), bf16[32,24,1024]{2,1,0:T(8,128)(2,1)}, u32[]{:S(2)}, u32[]{:S(2)}) async-start(bf16[32,24,1024]{2,1,0:T(8,128)(2,1)} %bitcast.46), calls=%async_computation.3 | async-start | bytes 3145728 | tf_op jit(solution)/shard_map/all_to_all | solution.py:324
  121.2 3.2 %copy-start.17 = (bf16[512,384]{1,0:T(8,128)(2,1)S(1)}, bf16[512,384]{1,0:T(8,128)(2,1)}, u32[]{:S(2)}) copy-start(bf16[512,384]{1,0:T(8,128)(2,1)} %get-tuple-element.49) | copy-start | bytes 1179652
  121.2 3.2 %copy-start.18 = (bf16[512,384]{1,0:T(8,128)(2,1)S(1)}, bf16[512,384]{1,0:T(8,128)(2,1)}, u32[]{:S(2)}) copy-start(bf16[512,384]{1,0:T(8,128)(2,1)} %get-tuple-element.50) | copy-start | bytes 1179652
  121.2 3.2 %copy-start.19 = (bf16[512,1536]{1,0:T(8,128)(2,1)S(1)}, bf16[512,1536]{1,0:T(8,128)(2,1)}, u32[]{:S(2)}) copy-start(bf16[512,1536]{1,0:T(8,128)(2,1)} %fusion) | copy-start | bytes 4718596
  124.3 11.2 %collective-permute-start.13 = (bf16[512,384]{1,0:T(8,128)(2,1)S(1)}, bf16[512,384]{1,0:T(8,128)(2,1)S(1)}, u32[]{:S(2)}, u32[]{:S(2)}) collective-permute-start(bf16[512,384]{1,0:T(8,128)(2,1)S(1)} %select_convert_fusion), channel_id=1, source_target_pairs={{0,1},{1,0},{2,3},{3,2},{4,5},{5,4},{6,7},{7,6},{8,9},{9,8},{10,11... | collective-permute-start | bytes 1179656 | tf_op jit(solution)/shard_map/ppermute | solution.py:376
  127.3 15.1 %copy-start.6 = (f32[96,1024]{1,0:T(8,128)S(1)}, f32[96,1024]{1,0:T(8,128)}, u32[]{:S(2)}) copy-start(f32[96,1024]{1,0:T(8,128)} %copy-done.5) | copy-start | bytes 1179652
  127.3 15.1 %copy-start.8 = (f32[96,512]{1,0:T(8,128)S(1)}, f32[96,512]{1,0:T(8,128)}, u32[]{:S(2)}) copy-start(f32[96,512]{1,0:T(8,128)} %copy-done.7) | copy-start | bytes 589828
  127.3 15.1 %copy-start.10 = (f32[96,512]{1,0:T(8,128)S(1)}, f32[96,512]{1,0:T(8,128)}, u32[]{:S(2)}) copy-start(f32[96,512]{1,0:T(8,128)} %copy-done.9) | copy-start | bytes 589828
  137.7 14.0 %collective-permute-start.10 = (bf16[192,512]{1,0:T(8,128)(2,1)S(1)}, bf16[192,512]{1,0:T(8,128)(2,1)S(1)}, u32[]{:S(2)}, u32[]{:S(2)}) collective-permute-start(bf16[192,512]{1,0:T(8,128)(2,1)S(1)} %get-tuple-element.42), channel_id=1, source_target_pairs={{0,32},{16,48},{32,0},{48,16},{1,33},{17,49},{33,1},{49,17},{2,34}... | collective-permute-start | bytes 589832 | tf_op jit(solution)/shard_map/ppermute | solution.py:314
  139.4 14.8 %collective-permute-start.11 = (bf16[192,512]{1,0:T(8,128)(2,1)S(1)}, bf16[192,512]{1,0:T(8,128)(2,1)S(1)}, u32[]{:S(2)}, u32[]{:S(2)}) collective-permute-start(bf16[192,512]{1,0:T(8,128)(2,1)S(1)} %get-tuple-element.43), channel_id=1, source_target_pairs={{0,48},{16,0},{32,16},{48,32},{1,49},{17,1},{33,17},{49,33},{2,50}... | collective-permute-start | bytes 589832 | tf_op jit(solution)/shard_map/ppermute | solution.py:314
  141.2 17.1 %collective-permute-start.9 = (bf16[192,512]{1,0:T(8,128)(2,1)S(1)}, bf16[192,512]{1,0:T(8,128)(2,1)S(1)}, u32[]{:S(2)}, u32[]{:S(2)}) collective-permute-start(bf16[192,512]{1,0:T(8,128)(2,1)S(1)} %get-tuple-element.41), channel_id=1, source_target_pairs={{0,16},{16,32},{32,48},{48,0},{1,17},{17,33},{33,49},{49,1},{2,18}... | collective-permute-start | bytes 589832 | tf_op jit(solution)/shard_map/ppermute | solution.py:314
  (6 other events, 5.1 us)
